TPU v7x, 1024 devices: a whole 4x8x16 slice. The times are simulated.
1024 devices in a mesh: gx: 32 (over y, x), gy: 8 (over z_lo), gz: 4 (over z_hi, core).
Axes of the slice: x: 4, y: 8, z: 16 (z_hi: 2, z_lo: 8; z = z_hi * 8 + z_lo), core: 2. Of those that a mesh axis runs over, the one named last changes fastest.
Arguments:
- pair_blocks: float32 [529, 32768], P(None, ('gx', 'gy', 'gz')), may hold values from -6 to 6
- basis_map: float32 [529, 64], replicated, may hold values from -0.25 to 0.25
- pair_cells: int32 [3, 32768], P(None, ('gx', 'gy', 'gz')), may hold values from 0 to 511, as said below
- pair_offsets: float32 [3, 32768], P(None, ('gx', 'gy', 'gz')), may hold values from 0 to 1
- exponent_index: int32 [32768], P(('gx', 'gy', 'gz')), may hold values from 0 to 15
- radius_index: int32 [32768], P(('gx', 'gy', 'gz')), may hold values from 0 to 4
- exponents: float32 [16], replicated, may hold values from 7 to 9
Outputs:
- density: float32 [256, 256, 512], P('gx', 'gy', 'gz')
- spectrum: float32 [2, 512, 256, 256], P(None, ('gy', 'gz'), 'gx')
Inputs may be any that keep to these rules, and one draw needn't show every extreme that they name: The y of pair_cells column p lies among the 32 cells, and its z among the 128 cells, of the gy and gz index of the device that holds column p. Of the pairs that one device holds at most 2 have x in the same run of 8 cells that one gx index holds, and in every draw some such run gets exactly 2 from every device.
All inputs are finite; a program needn't handle non-finite values.
Results may differ from a plain program's by a relative error of at most 0.0003.
Values sent between devices are 32-bit elements; how exact they have to be, the bound alone decides.
A program may use at most 32 MiB of HBM per device.

v0:
```python
import math

import jax
import jax.numpy as jnp
import ml_dtypes
import numpy as np
from jax import lax
from jax.experimental import pallas as pl
from jax.experimental.pallas import tpu as pltpu
from jax.sharding import PartitionSpec as P

HALO = 8
CX, CY, CZ = 8, 32, 128
GX, GY, GZ = 32, 8, 4
RING = GY * GZ
NZ = GZ * CZ
NXY = 256
SLOTS = GX * 8
GROUPS = 6
SLAB = 72
MESH = pl.DeviceIdType.MESH
F32 = jnp.float32
BF16 = jnp.bfloat16

NN = (((1,), (0,)), ((), ()))
NT = (((1,), (1,)), ((), ()))
TN = (((0,), (0,)), ((), ()))


def halves(value):
    high = value.astype(BF16)
    return high, (value - high.astype(F32)).astype(BF16)


def dot(a, b, dims):
    return lax.dot_general(a, b, dims, preferred_element_type=F32)


def dot3(a, b, dims):
    return dot(a[0], b[0], dims) + (dot(a[0], b[1], dims) + dot(a[1], b[0], dims))


def np_halves(value):
    value = value.astype(np.float32)
    high = value.astype(ml_dtypes.bfloat16)
    return high, (value - high.astype(np.float32)).astype(ml_dtypes.bfloat16)


def depth_matrix():
    lane = np.arange(128)
    kz = 16 * (8 * np.arange(4)[:, None] + lane[None, :] % 8) + lane[None, :] // 8
    phase = np.arange(NZ)[:, None] * kz.reshape(-1)[None, :] % NZ
    angle = phase * (2.0 * math.pi / NZ)
    scale = 1.0 / math.sqrt(NZ)
    return np.concatenate([np.cos(angle) * scale, -np.sin(angle) * scale], 1)


def plane_matrices():
    index = np.arange(NXY)
    angle = (index[:, None] * index[None, :] % NXY) * (2.0 * math.pi / NXY)
    scale = 1.0 / math.sqrt(NXY)
    return np.cos(angle) * scale, np.sin(angle) * scale


def iota(shape, axis):
    return lax.broadcasted_iota(jnp.int32, shape, axis)


def swap_lanes(v, count, group):
    bit = 1
    while bit < count:
        shift = bit * group
        v = v.reshape(count // (2 * bit), 2, bit * 8, 128)
        a = v[:, 0].reshape(count * 4, 128)
        c = v[:, 1].reshape(count * 4, 128)
        low = (iota((count * 4, 128), 1) // shift) % 2 == 0
        na = jnp.where(low, a, pltpu.roll(c, shift, 1))
        nc = jnp.where(low, pltpu.roll(a, 128 - shift, 1), c)
        parts = (count // (2 * bit), 1, bit * 8, 128)
        v = jnp.concatenate([na.reshape(parts), nc.reshape(parts)], 1)
        v = v.reshape(count, 8, 128)
        bit *= 2
    return v


def kernel(
    blocks_ref, basis_ref, cells_ref, offsets_ref, eidx_ref, ridx_ref, exps_ref,
    wz_hbm, wxy_hbm, dens_ref, spec_ref,
    wz, wxy, out1, recv1, amps, t_hi, t_lo, slabs, main_in, rim_in, lines,
    out4, in4, out5, in5, dens_in,
    wsem, s1, r1, s3, r3, r3x, s4, r4, s5, r5, sd, rd,
):
    gx, gy, gz = lax.axis_index("gx"), lax.axis_index("gy"), lax.axis_index("gz")
    me = gy * GZ + gz

    def plane_peer(target):
        return {"gx": target}

    def ring_peer(target):
        return {"gy": target // GZ, "gz": target % GZ}

    wz_copy = pltpu.make_async_copy(wz_hbm, wz, wsem.at[0])
    wxy_copy = pltpu.make_async_copy(wxy_hbm, wxy, wsem.at[1])
    wz_copy.start()
    wxy_copy.start()

    barrier = pltpu.get_barrier_semaphore()

    @pl.loop(1, GX)
    def _(d):
        pl.semaphore_signal(
            barrier, inc=1, device_id=plane_peer(lax.rem(gx + d, GX)), device_id_type=MESH
        )

    @pl.loop(1, RING)
    def _(d):
        pl.semaphore_signal(
            barrier, inc=1, device_id=ring_peer(lax.rem(me + d, RING)), device_id_type=MESH
        )

    coefs = dot3(halves(basis_ref[...]), halves(blocks_ref[...]), TN)
    cells = cells_ref[...].astype(F32)
    radius = (HALO - ridx_ref[...]).astype(F32)
    rate = jnp.zeros((1, 32), F32)
    for e in range(16):
        rate = rate + jnp.where(eidx_ref[...] == e, exps_ref[e], 0.0)
    rate = rate / (radius * radius)
    data = jnp.concatenate(
        [coefs, cells, offsets_ref[...], rate, radius, jnp.zeros((56, 32), F32)], 0
    )
    owner = cells_ref[0:1, :] // CX
    same_pair = iota((32, 32), 0) == iota((32, 32), 1)
    owner_column = jnp.sum(
        jnp.where(same_pair, owner.astype(F32), 0.0), axis=1, keepdims=True
    ).astype(jnp.int32)
    earlier = (owner_column == owner) & (iota((32, 32), 0) < iota((32, 32), 1))
    within = jnp.sum(jnp.where(earlier, 1.0, 0.0), axis=0, keepdims=True).astype(jnp.int32)
    base = owner * 2 + within
    row = iota((SLOTS, 1), 0)
    slot = row % 8
    code = (row // 8 + slot // 2 + (GX - 1)) % GX * 2 + slot % 2
    code = jnp.where(slot < 6, code, -1)
    pick = jnp.where(code == base, 1.0, 0.0).astype(BF16)
    high, middle = halves(data)
    rest = (data - high.astype(F32) - middle.astype(F32)).astype(BF16)
    routed = dot(pick, high, NT) + dot(pick, middle, NT) + dot(pick, rest, NT)
    out1[...] = routed.reshape(GX, 8, 128)
    recv1[gx] = out1[gx]

    pl.semaphore_wait(barrier, GX + RING - 2)

    def copy1(target, source):
        return pltpu.make_async_remote_copy(
            src_ref=out1.at[target], dst_ref=recv1.at[source],
            send_sem=s1.at[target], recv_sem=r1.at[source],
            device_id=plane_peer(target), device_id_type=MESH,
        )

    @pl.loop(1, GX)
    def _(d):
        copy1(lax.rem(gx + d, GX), gx).start()

    @pl.loop(1, GX)
    def _(d):
        other = lax.rem(gx + d, GX)
        copy1(other, other).wait_recv()

    table = recv1[...].reshape(SLOTS, 128).T
    cx, cy, cz = table[64:65], table[65:66], table[66:67]
    ox, oy, oz = table[67:68], table[68:69], table[69:70]
    rates, radii = table[70:71], table[71:72]

    def factors(offset_cells, offset_in):
        distance = offset_cells - offset_in
        inside = jnp.abs(offset_cells) <= radii
        envelope = jnp.where(inside, jnp.exp(-rates * distance * distance), 0.0)
        scaled = distance * (1.0 / HALO)
        first = envelope * scaled
        second = first * scaled
        return [envelope, first, second, second * scaled]

    step_x = (gx * CX + iota((CX, 1), 0)).astype(F32) - cx
    step_x = jnp.where(step_x > 128.0, step_x - 256.0, step_x)
    step_x = jnp.where(step_x < -128.0, step_x + 256.0, step_x)
    along_x = factors(step_x, ox)
    for j in range(4):
        for k in range(4):
            total = table[j * 4 + k : j * 4 + k + 1] * along_x[0]
            for i in range(1, 4):
                at = i * 16 + j * 4 + k
                total = total + table[at : at + 1] * along_x[i]
            amps[j * 4 + k] = total
    along_y = factors((gy * CY - HALO + iota((48, 1), 0)).astype(F32) - cy, oy)
    z_row = iota((256, 1), 0)
    rim = z_row % 16
    z_cell = jnp.where(
        z_row < CZ, z_row, jnp.where(rim < HALO, CZ + rim, rim - 2 * HALO)
    )
    along_z = factors((gz * CZ + z_cell).astype(F32) - cz, oz)

    for x in range(CX):
        for k in range(4):
            total = amps[k, x : x + 1, :] * along_y[0]
            for j in range(1, 4):
                total = total + amps[j * 4 + k, x : x + 1, :] * along_y[j]
            high, low = halves(total)
            t_hi[x * 48 : (x + 1) * 48, k * SLOTS : (k + 1) * SLOTS] = high
            t_lo[x * 48 : (x + 1) * 48, k * SLOTS : (k + 1) * SLOTS] = low
    z_all = halves(jnp.concatenate(along_z, 1))
    block = dot3((t_hi[...], t_lo[...]), z_all, NT)
    keep = iota((8, 128), 1) // 16 == iota((8, 128), 0)
    for x in range(CX):
        for g in range(GROUPS):
            at = x * 48 + g * 8
            slabs[g, x * 8 : (x + 1) * 8, :] = block[at : at + 8, :128]
            slabs[g, 64 + x : 65 + x, :] = jnp.sum(
                jnp.where(keep, block[at : at + 8, 128:], 0.0), axis=0, keepdims=True
            )

    def copy3(group, source):
        return pltpu.make_async_remote_copy(
            src_ref=slabs.at[group], dst_ref=main_in.at[source],
            send_sem=s3.at[group], recv_sem=r3.at[source],
            device_id={"gz": group - 1}, device_id_type=MESH,
        )

    def copy3_rim(group, source, row_to, depth_to):
        return pltpu.make_async_remote_copy(
            src_ref=slabs.at[group], dst_ref=rim_in.at[source],
            send_sem=s3.at[group], recv_sem=r3x.at[source],
            device_id={"gy": row_to, "gz": depth_to}, device_id_type=MESH,
        )

    before, after = lax.rem(gy + GY - 1, GY), lax.rem(gy + 1, GY)

    @pl.loop(1, GZ)
    def _(d):
        copy3(1 + lax.rem(gz + d, GZ), gz).start()

    copy3_rim(0, gz, before, GZ - 1).start()
    copy3_rim(5, gz, after, 0).start()
    main_in[gz] = slabs[1 + gz]

    edge = (gz == 0) | (gz == GZ - 1)

    @pl.when(jnp.logical_not(edge))
    def _():
        rim_in[...] = jnp.zeros((GZ, SLAB, 128), F32)

    wz_copy.wait()
    wxy_copy.wait()

    @pl.loop(1, GZ)
    def _(d):
        other = lax.rem(gz + d, GZ)
        copy3(1 + other, other).wait_recv()

    @pl.when(edge)
    def _():
        @pl.loop(0, GZ)
        def _(source):
            copy3_rim(0, source, before, GZ - 1).wait_recv()

    row_lane = iota((64, 128), 1)
    keep_rows = row_lane // 16 == iota((64, 128), 0) % 8
    rims = []
    for q in range(GZ):
        packed = main_in[q, 64:SLAB, :] + rim_in[q, 64:SLAB, :]
        spread = jnp.concatenate(
            [jnp.broadcast_to(packed[x : x + 1], (8, 128)) for x in range(CX)], 0
        )
        spread = jnp.where(keep_rows, spread, 0.0)
        for shift in (16, 32, 64):
            spread = spread + pltpu.roll(spread, shift, 1)
        rims.append(spread)
    for q in range(GZ):
        lines[q] = (
            main_in[q, 0:64, :]
            + rim_in[q, 0:64, :]
            + jnp.where(row_lane >= CZ - HALO, rims[(q + 1) % GZ], 0.0)
            + jnp.where(row_lane < HALO, rims[(q + GZ - 1) % GZ], 0.0)
        )
    line_parts = halves(jnp.concatenate([lines[q] for q in range(GZ)], 1))
    for c in range(8):
        columns = slice(c * 128, (c + 1) * 128)
        part = dot3(line_parts, (wz[0, :, columns], wz[1, :, columns]), NN)
        part = swap_lanes(part.reshape(8, 8, 128), 8, 1)
        first = c % 4 * 8
        out4[first : first + 8, c // 4] = part

    def copy4(target, source):
        return pltpu.make_async_remote_copy(
            src_ref=out4.at[target], dst_ref=in4.at[:, pl.ds(pl.multiple_of(source * 8, 8), 8), :],
            send_sem=s4.at[target], recv_sem=r4.at[source],
            device_id=ring_peer(target), device_id_type=MESH,
        )

    @pl.loop(1, RING)
    def _(d):
        copy4(lax.rem(me + d, RING), me).start()

    def copy_d(target, source):
        return pltpu.make_async_remote_copy(
            src_ref=lines.at[target], dst_ref=dens_in.at[source],
            send_sem=sd.at[target], recv_sem=rd.at[source],
            device_id={"gz": target}, device_id_type=MESH,
        )

    @pl.loop(1, GZ)
    def _(d):
        copy_d(lax.rem(gz + d, GZ), gz).start()

    in4[:, pl.ds(pl.multiple_of(me * 8, 8), 8), :] = out4[me]
    dens_in[gz] = lines[gz]

    @pl.loop(1, RING)
    def _(d):
        other = lax.rem(me + d, RING)
        copy4(other, other).wait_recv()

    cosines = (wxy[0], wxy[1])
    sines = (wxy[2], wxy[3])
    rows_in = halves(jnp.concatenate([in4[0], in4[1]], 1))
    with_cos = dot3(cosines, rows_in, NN)
    with_sin = dot3(sines, rows_in, NN)
    out5[0] = with_cos[:, :128] + with_sin[:, 128:]
    out5[1] = with_cos[:, 128:] - with_sin[:, :128]

    def copy5(target, source):
        return pltpu.make_async_remote_copy(
            src_ref=out5.at[:, pl.ds(pl.multiple_of(target * 8, 8), 8), :], dst_ref=in5.at[source],
            send_sem=s5.at[target], recv_sem=r5.at[source],
            device_id=plane_peer(target), device_id_type=MESH,
        )

    @pl.loop(1, GX)
    def _(d):
        copy5(lax.rem(gx + d, GX), gx).start()

    in5[gx] = out5[:, pl.ds(pl.multiple_of(gx * 8, 8), 8), :]

    @pl.loop(1, GX)
    def _(d):
        other = lax.rem(gx + d, GX)
        copy5(other, other).wait_recv()

    sides = []
    for part in range(2):
        pieces = [
            swap_lanes(in5[h * 16 : (h + 1) * 16, part], 16, 8).reshape(128, 128)
            for h in range(2)
        ]
        sides.append(jnp.concatenate(pieces, 1))
    x_lines = halves(jnp.concatenate(sides, 0))
    with_cos = dot3(x_lines, cosines, NN)
    with_sin = dot3(x_lines, sines, NN)
    spec_ref[0] = (with_cos[:128] + with_sin[128:]).reshape(16, 8, NXY)
    spec_ref[1] = (with_cos[128:] - with_sin[:128]).reshape(16, 8, NXY)

    @pl.loop(1, GZ)
    def _(d):
        other = lax.rem(gz + d, GZ)
        copy_d(other, other).wait_recv()

    for q in range(GZ):
        dens_ref[:, q * 8 : (q + 1) * 8, :] = dens_in[q].reshape(8, 8, 128)

    @pl.loop(1, GX)
    def _(d):
        other = lax.rem(gx + d, GX)
        copy1(other, gx).wait_send()
        copy5(other, gx).wait_send()

    @pl.loop(1, RING)
    def _(d):
        copy4(lax.rem(me + d, RING), me).wait_send()

    @pl.loop(1, GZ)
    def _(d):
        other = lax.rem(gz + d, GZ)
        copy3(1 + other, gz).wait_send()
        copy_d(other, gz).wait_send()

    copy3_rim(0, gz, before, GZ - 1).wait_send()
    copy3_rim(5, gz, after, 0).wait_send()


def solution(mesh):
    wz = np.stack(np_halves(depth_matrix()))
    cos_m, sin_m = plane_matrices()
    wxy = np.stack([*np_halves(cos_m), *np_halves(sin_m)])
    vmem = pl.BlockSpec(memory_space=pltpu.VMEM)
    anywhere = pl.BlockSpec(memory_space=pl.ANY)
    dma = pltpu.SemaphoreType.DMA
    call = pl.pallas_call(
        kernel,
        out_shape=(
            jax.ShapeDtypeStruct((CX, CY, CZ), F32),
            jax.ShapeDtypeStruct((2, 16, 8, NXY), F32),
        ),
        in_specs=[vmem] * 6 + [pl.BlockSpec(memory_space=pltpu.SMEM), anywhere, anywhere],
        out_specs=(vmem, vmem),
        scratch_shapes=[
            pltpu.VMEM((2, NZ, 2 * NZ), BF16),
            pltpu.VMEM((4, NXY, NXY), BF16),
            pltpu.VMEM((GX, 8, 128), F32),
            pltpu.VMEM((GX, 8, 128), F32),
            pltpu.VMEM((16, 8, SLOTS), F32),
            pltpu.VMEM((384, 4 * SLOTS), BF16),
            pltpu.VMEM((384, 4 * SLOTS), BF16),
            pltpu.VMEM((GROUPS, SLAB, 128), F32),
            pltpu.VMEM((GZ, SLAB, 128), F32),
            pltpu.VMEM((GZ, SLAB, 128), F32),
            pltpu.VMEM((GZ, 64, 128), F32),
            pltpu.VMEM((RING, 2, 8, 128), F32),
            pltpu.VMEM((2, NXY, 128), F32),
            pltpu.VMEM((2, NXY, 128), F32),
            pltpu.VMEM((GX, 2, 8, 128), F32),
            pltpu.VMEM((GZ, 64, 128), F32),
            dma((2,)),
            dma((GX,)), dma((GX,)),
            dma((GROUPS,)), dma((GZ,)), dma((GZ,)),
            dma((RING,)), dma((RING,)),
            dma((GX,)), dma((GX,)),
            dma((GZ,)), dma((GZ,)),
        ],
        compiler_params=pltpu.CompilerParams(collective_id=0, has_side_effects=True),
        name="pair_grid_transform",
    )

    def shards(blocks, basis, cells, offsets, eidx, ridx, exps):
        return call(
            blocks, basis, cells, offsets, eidx.reshape(1, -1), ridx.reshape(1, -1), exps,
            jnp.asarray(wz), jnp.asarray(wxy),
        )

    split = ("gx", "gy", "gz")
    placed = (P(None, split), P(), P(None, split), P(None, split), P(split), P(split), P())
    return jax.shard_map(
        shards,
        mesh=mesh,
        in_specs=placed,
        out_specs=(P("gx", "gy", "gz"), P(None, ("gy", "gz"), "gx", None)),
        check_vma=False,
    )
```

profile of v0, /device:TPU:1, one launch (start us, length us, event | category | flops | bytes accessed | tf_op | source)
XLA Modules:
  0.0 85.9 jit_solution(8371272668266659938)
XLA Ops:
  0.6 1.7 %copy.11.blocks_ref = f32[529,32]{1,0:T(8,128)} copy(f32[529,32]{0,1:T(8,128)} %param.9) | data formatting | bytes 135424 | tf_op args[0]
  2.4 1.8 %copy.12.basis_ref = f32[529,64]{1,0:T(8,128)} copy(f32[529,64]{0,1:T(8,128)} %param.10) | data formatting | bytes 270848 | tf_op args[1]
  4.1 78.5 %pair_grid_transform.1 = (f32[8,32,128]{2,1,0:T(8,128)}, f32[2,16,8,256]{3,2,1,0:T(8,128)}) custom-call(f32[529,32]{1,0:T(8,128)} %copy.11.blocks_ref, f32[529,64]{1,0:T(8,128)} %copy.12.basis_ref, s32[3,32]{1,0:T(4,128)} %cells_ref.1, f32[3,32]{1,0:T(4,128)} %offsets_ref.1, s32[1,32]{1,0:T(1,128)} %bitcast.2, s32[1,32]{1,0:T(1,128)} %bitcast.3, ...), custom_call_target="tpu_custom_call" | custom-call | tf_op jit(solution)/shard_map/pair_grid_transform/pallas_call | solution.py:432
  82.6 1.6 %copy.15 = f32[8,32,128]{2,1,0:T(8,128)} copy(f32[8,32,128]{2,1,0:T(8,128)} %get-tuple-element.4) | data formatting | bytes 262144
  84.2 1.7 %copy.16 = f32[2,16,8,256]{3,2,1,0:T(8,128)} copy(f32[2,16,8,256]{3,2,1,0:T(8,128)} %get-tuple-element.5) | data formatting | bytes 524288
where the time goes:
time: 87.1 us; the launch traced here: 85.9 us
  Pallas kernels  78.5 us (90%)
  local copies, waits for them, and re-layouts  6.73 us (8%)
    pallas_call x1, Pallas kernels, shards(): call(blocks, basis, cells, offsets, eidx.reshape(1, -1), ridx.reshape(1,...  78.5 us
    unnamed x4, local copies, waits for them, and re-layouts  6.73 us

commit v1 on v0

--- a/solution.py
+++ b/solution.py
@@ -24,7 +24,6 @@
 
 NN = (((1,), (0,)), ((), ()))
 NT = (((1,), (1,)), ((), ()))
-TN = (((0,), (0,)), ((), ()))
 
 
 def halves(value):
@@ -93,6 +92,19 @@
     gx, gy, gz = lax.axis_index("gx"), lax.axis_index("gy"), lax.axis_index("gz")
     me = gy * GZ + gz
 
+    half, core = gz // 2, gz % 2
+
+    def far_first(i, reach):
+        return (reach - (i + 1) // 2) * (2 * (i % 2) - 1)
+
+    def plane_step(i):
+        row = lax.rem(gx // 4 + far_first(i // 4, 4) + 8, 8)
+        return row * 4 + lax.rem(gx % 4 + far_first(i % 4, 2) + 4, 4)
+
+    def ring_step(i):
+        depth = lax.rem(gy + 8 * half + far_first(i // 2, 8) + 16, 16)
+        return depth % 8 * GZ + depth // 8 * 2 + (core + 1 + i) % 2
+
     def plane_peer(target):
         return {"gx": target}
 
@@ -106,19 +118,19 @@
 
     barrier = pltpu.get_barrier_semaphore()
 
-    @pl.loop(1, GX)
-    def _(d):
+    @pl.loop(0, GX - 1)
+    def _(i):
         pl.semaphore_signal(
-            barrier, inc=1, device_id=plane_peer(lax.rem(gx + d, GX)), device_id_type=MESH
-        )
-
-    @pl.loop(1, RING)
-    def _(d):
+            barrier, inc=1, device_id=plane_peer(plane_step(i)), device_id_type=MESH
+        )
+
+    @pl.loop(0, RING - 1)
+    def _(i):
         pl.semaphore_signal(
-            barrier, inc=1, device_id=ring_peer(lax.rem(me + d, RING)), device_id_type=MESH
-        )
-
-    coefs = dot3(halves(basis_ref[...]), halves(blocks_ref[...]), TN)
+            barrier, inc=1, device_id=ring_peer(ring_step(i)), device_id_type=MESH
+        )
+
+    coefs = dot3(halves(basis_ref[...]), halves(blocks_ref[...]), NT)
     cells = cells_ref[...].astype(F32)
     radius = (HALO - ridx_ref[...]).astype(F32)
     rate = jnp.zeros((1, 32), F32)
@@ -156,9 +168,9 @@
             device_id=plane_peer(target), device_id_type=MESH,
         )
 
-    @pl.loop(1, GX)
-    def _(d):
-        copy1(lax.rem(gx + d, GX), gx).start()
+    @pl.loop(0, GX - 1)
+    def _(i):
+        copy1(plane_step(i), gx).start()
 
     @pl.loop(1, GX)
     def _(d):
@@ -233,12 +245,11 @@
 
     before, after = lax.rem(gy + GY - 1, GY), lax.rem(gy + 1, GY)
 
-    @pl.loop(1, GZ)
-    def _(d):
-        copy3(1 + lax.rem(gz + d, GZ), gz).start()
-
+    copy3(3 - 2 * half + core, gz).start()
+    copy3(4 - 2 * half - core, gz).start()
     copy3_rim(0, gz, before, GZ - 1).start()
     copy3_rim(5, gz, after, 0).start()
+    copy3(2 + 2 * half - core, gz).start()
     main_in[gz] = slabs[1 + gz]
 
     edge = (gz == 0) | (gz == GZ - 1)
@@ -295,9 +306,9 @@
             device_id=ring_peer(target), device_id_type=MESH,
         )
 
-    @pl.loop(1, RING)
-    def _(d):
-        copy4(lax.rem(me + d, RING), me).start()
+    @pl.loop(0, RING - 1)
+    def _(i):
+        copy4(ring_step(i), me).start()
 
     def copy_d(target, source):
         return pltpu.make_async_remote_copy(
@@ -305,10 +316,6 @@
             send_sem=sd.at[target], recv_sem=rd.at[source],
             device_id={"gz": target}, device_id_type=MESH,
         )
-
-    @pl.loop(1, GZ)
-    def _(d):
-        copy_d(lax.rem(gz + d, GZ), gz).start()
 
     in4[:, pl.ds(pl.multiple_of(me * 8, 8), 8), :] = out4[me]
     dens_in[gz] = lines[gz]
@@ -333,9 +340,13 @@
             device_id=plane_peer(target), device_id_type=MESH,
         )
 
-    @pl.loop(1, GX)
-    def _(d):
-        copy5(lax.rem(gx + d, GX), gx).start()
+    @pl.loop(0, GX - 1)
+    def _(i):
+        copy5(plane_step(i), gx).start()
+
+    @pl.loop(1, GZ)
+    def _(d):
+        copy_d(lax.rem(gz + d, GZ), gz).start()
 
     in5[gx] = out5[:, pl.ds(pl.multiple_of(gx * 8, 8), 8), :]
 
@@ -430,7 +441,7 @@
 
     def shards(blocks, basis, cells, offsets, eidx, ridx, exps):
         return call(
-            blocks, basis, cells, offsets, eidx.reshape(1, -1), ridx.reshape(1, -1), exps,
+            blocks.T, basis.T, cells, offsets, eidx.reshape(1, -1), ridx.reshape(1, -1), exps,
             jnp.asarray(wz), jnp.asarray(wxy),
         )
 

time: 87.1 us -> 80.2 us (0.921); the launches traced: 85.9 us -> 80 us
  local copies, waits for them, and re-layouts: 6.73 us -> 3.24 us
  Pallas kernels: 78.5 us -> 76.1 us
    unnamed x4 -> x2, local copies, waits for them, and re-layouts: 6.73 us -> 3.24 us
    pallas_call x1, Pallas kernels: 78.5 us -> 76.1 us  [shards(): call(blocks.T, basis.T, cells, offsets, eidx.reshape(1, -1), ridx.reshape...]
where the time goes in v1:
time: 80.2 us; the launch traced here: 80 us
  Pallas kernels  76.1 us (95%)
  local copies, waits for them, and re-layouts  3.24 us (4%)
    pallas_call x1, Pallas kernels, shards(): call(blocks.T, basis.T, cells, offsets, eidx.reshape(1, -1), ridx.reshape...  76.1 us
    unnamed x2, local copies, waits for them, and re-layouts  3.24 us

profile of v1, /device:TPU:1, one launch (start us, length us, event | category | flops | bytes accessed | tf_op | source)
XLA Modules:
  0.0 80.0 jit_solution(7615176248924522154)
XLA Ops:
  0.6 76.1 %pair_grid_transform.1 = (f32[8,32,128]{2,1,0:T(8,128)}, f32[2,16,8,256]{3,2,1,0:T(8,128)}) custom-call(f32[32,529]{1,0:T(8,128)} %bitcast.5, f32[64,529]{1,0:T(8,128)} %bitcast.4, s32[3,32]{1,0:T(4,128)} %cells_ref.1, f32[3,32]{1,0:T(4,128)} %offsets_ref.1, s32[1,32]{1,0:T(1,128)} %bitcast.6, s32[1,32]{1,0:T(1,128)} %bitcast.7, f32[16]{0:T(128)} %exps_ref.1, ...), custom_call_target="tpu_custom_call" | custom-call | tf_op jit(solution)/shard_map/pair_grid_transform/pallas_call | solution.py:443
  76.8 1.6 %copy.13 = f32[8,32,128]{2,1,0:T(8,128)} copy(f32[8,32,128]{2,1,0:T(8,128)} %get-tuple-element.4) | data formatting | bytes 262144
  78.4 1.7 %copy.14 = f32[2,16,8,256]{3,2,1,0:T(8,128)} copy(f32[2,16,8,256]{3,2,1,0:T(8,128)} %get-tuple-element.5) | data formatting | bytes 524288

commit v2 on v1

v2 whole, which is shorter than its diff:
```python
import math

import jax
import jax.numpy as jnp
import ml_dtypes
import numpy as np
from jax import lax
from jax.experimental import pallas as pl
from jax.experimental.pallas import tpu as pltpu
from jax.sharding import PartitionSpec as P

HALO = 8
CX, CY, CZ = 8, 32, 128
GX, GY, GZ = 32, 8, 4
RING = GY * GZ
NZ = GZ * CZ
NXY = 256
SLOTS = GX * 8
GROUPS = 6
SLAB = 36
HX = 4
MESH = pl.DeviceIdType.MESH
F32 = jnp.float32
BF16 = jnp.bfloat16

NN = (((1,), (0,)), ((), ()))
NT = (((1,), (1,)), ((), ()))


def halves(value):
    high = value.astype(BF16)
    return high, (value - high.astype(F32)).astype(BF16)


def dot(a, b, dims):
    return lax.dot_general(a, b, dims, preferred_element_type=F32)


def dot3(a, b, dims):
    rows = a[0].shape[0]
    both = dot(jnp.concatenate(a, 0), b[0], dims)
    return both[:rows] + (both[rows:] + dot(a[0], b[1], dims))


def unrolled(count):
    def run(body):
        for i in range(count):
            body(i)

    return run


def np_halves(value):
    value = value.astype(np.float32)
    high = value.astype(ml_dtypes.bfloat16)
    return high, (value - high.astype(np.float32)).astype(ml_dtypes.bfloat16)


def depth_matrix():
    lane = np.arange(128)
    kz = 16 * (8 * np.arange(4)[:, None] + lane[None, :] % 8) + lane[None, :] // 8
    phase = np.arange(NZ)[:, None] * kz.reshape(-1)[None, :] % NZ
    angle = phase * (2.0 * math.pi / NZ)
    scale = 1.0 / math.sqrt(NZ)
    return np.concatenate([np.cos(angle) * scale, -np.sin(angle) * scale], 1)


def plane_matrices():
    index = np.arange(NXY)
    angle = (index[:, None] * index[None, :] % NXY) * (2.0 * math.pi / NXY)
    scale = 1.0 / math.sqrt(NXY)
    order = np.arange(NXY).reshape(GX, 2, HX).transpose(1, 0, 2).reshape(-1)
    cosine, sine = np.cos(angle) * scale, np.sin(angle) * scale
    return cosine, sine, cosine[order], sine[order]


def iota(shape, axis):
    return lax.broadcasted_iota(jnp.int32, shape, axis)


def swap_lanes(v, count, group):
    bit = 1
    while bit < count:
        shift = bit * group
        v = v.reshape(count // (2 * bit), 2, bit * 8, 128)
        a = v[:, 0].reshape(count * 4, 128)
        c = v[:, 1].reshape(count * 4, 128)
        low = (iota((count * 4, 128), 1) // shift) % 2 == 0
        na = jnp.where(low, a, pltpu.roll(c, shift, 1))
        nc = jnp.where(low, pltpu.roll(a, 128 - shift, 1), c)
        parts = (count // (2 * bit), 1, bit * 8, 128)
        v = jnp.concatenate([na.reshape(parts), nc.reshape(parts)], 1)
        v = v.reshape(count, 8, 128)
        bit *= 2
    return v


def kernel(
    blocks_ref, basis_ref, cells_ref, offsets_ref, eidx_ref, ridx_ref, exps_ref,
    wz_hbm, wxy_hbm, dens_ref, spec_ref,
    wz, wxy, out1, recv1, amps, t_hi, t_lo, slabs, main_in, rim_in, lines,
    out4, in4, out5, in5, dens_in,
    wsem, s1, r1, s3, r3, r3x, s4, r4, s5, r5, sd, rd,
):
    gx, gy, gz = lax.axis_index("gx"), lax.axis_index("gy"), lax.axis_index("gz")
    me = gy * GZ + gz

    half, core = gz >> 1, gz & 1

    def far_first(i, reach):
        return (reach - (i + 1) // 2) * (2 * (i % 2) - 1)

    def plane_step(i):
        row = ((gx >> 2) + far_first(i // 4, 4)) & 7
        return row * 4 + (((gx & 3) + far_first(i % 4, 2)) & 3)

    def ring_step(i):
        depth = (gy + 8 * half + far_first(i // 2, 8)) & 15
        return (depth & 7) * GZ + (depth >> 3) * 2 + ((core + 1 + i) & 1)

    def arrived(ref, semaphore):
        pltpu.make_async_copy(ref, ref, semaphore).wait()

    def plane_peer(target):
        return {"gx": target}

    def ring_peer(target):
        return {"gy": target >> 2, "gz": target & 3}

    wz_copy = pltpu.make_async_copy(wz_hbm, wz, wsem.at[0])
    wxy_copy = pltpu.make_async_copy(wxy_hbm, wxy, wsem.at[1])
    wz_copy.start()
    wxy_copy.start()

    barrier = pltpu.get_barrier_semaphore()

    @unrolled(GX - 1)
    def _(i):
        pl.semaphore_signal(
            barrier, inc=1, device_id=plane_peer(plane_step(i)), device_id_type=MESH
        )

    @unrolled(RING - 1)
    def _(i):
        pl.semaphore_signal(
            barrier, inc=1, device_id=ring_peer(ring_step(i)), device_id_type=MESH
        )

    coefs = dot3(halves(basis_ref[...]), halves(blocks_ref[...]), NT)
    cells = cells_ref[...].astype(F32)
    radius = (HALO - ridx_ref[...]).astype(F32)
    rate = jnp.zeros((1, 32), F32)
    for e in range(16):
        rate = rate + jnp.where(eidx_ref[...] == e, exps_ref[e], 0.0)
    rate = rate / (radius * radius)
    data = jnp.concatenate(
        [coefs, cells, offsets_ref[...], rate, radius, jnp.zeros((56, 32), F32)], 0
    )
    owner = cells_ref[0:1, :] // CX
    same_pair = iota((32, 32), 0) == iota((32, 32), 1)
    owner_column = jnp.sum(
        jnp.where(same_pair, owner.astype(F32), 0.0), axis=1, keepdims=True
    ).astype(jnp.int32)
    earlier = (owner_column == owner) & (iota((32, 32), 0) < iota((32, 32), 1))
    within = jnp.sum(jnp.where(earlier, 1.0, 0.0), axis=0, keepdims=True).astype(jnp.int32)
    base = owner * 2 + within
    row = iota((SLOTS, 1), 0)
    slot = row % 8
    code = (row // 8 + slot // 2 + (GX - 1)) % GX * 2 + slot % 2
    code = jnp.where(slot < 6, code, -1)
    pick = jnp.where(code == base, 1.0, 0.0).astype(BF16)
    high, middle = halves(data)
    rest = (data - high.astype(F32) - middle.astype(F32)).astype(BF16)
    routed = dot(pick, high, NT) + dot(pick, middle, NT) + dot(pick, rest, NT)
    out1[...] = routed.reshape(GX, 8, 128)
    recv1[gx] = out1[gx]

    pl.semaphore_wait(barrier, GX + RING - 2)

    def copy1(target, source):
        return pltpu.make_async_remote_copy(
            src_ref=out1.at[target], dst_ref=recv1.at[source],
            send_sem=s1, recv_sem=r1,
            device_id=plane_peer(target), device_id_type=MESH,
        )

    @unrolled(GX - 1)
    def _(i):
        copy1(plane_step(i), gx).start()

    arrived(recv1.at[0 : GX - 1], r1)

    table = recv1[...].reshape(SLOTS, 128).T
    cx, cy, cz = table[64:65], table[65:66], table[66:67]
    ox, oy, oz = table[67:68], table[68:69], table[69:70]
    rates, radii = table[70:71], table[71:72]

    def factors(offset_cells, offset_in):
        distance = offset_cells - offset_in
        inside = jnp.abs(offset_cells) <= radii
        envelope = jnp.where(inside, jnp.exp(-rates * distance * distance), 0.0)
        scaled = distance * (1.0 / HALO)
        first = envelope * scaled
        second = first * scaled
        return [envelope, first, second, second * scaled]

    step_x = (gx * CX + iota((CX, 1), 0)).astype(F32) - cx
    step_x = jnp.where(step_x > 128.0, step_x - 256.0, step_x)
    step_x = jnp.where(step_x < -128.0, step_x + 256.0, step_x)
    along_x = factors(step_x, ox)
    for j in range(4):
        for k in range(4):
            total = table[j * 4 + k : j * 4 + k + 1] * along_x[0]
            for i in range(1, 4):
                at = i * 16 + j * 4 + k
                total = total + table[at : at + 1] * along_x[i]
            amps[j * 4 + k] = total
    along_y = factors((gy * CY - HALO + iota((48, 1), 0)).astype(F32) - cy, oy)
    z_row = iota((256, 1), 0)
    rim = z_row % 16
    z_cell = jnp.where(
        z_row < CZ, z_row, jnp.where(rim < HALO, CZ + rim, rim - 2 * HALO)
    )
    along_z = factors((gz * CZ + z_cell).astype(F32) - cz, oz)

    z_all = halves(jnp.concatenate(along_z, 1))
    keep = iota((8, 128), 1) // 16 == iota((8, 128), 0)

    def copy3(h, group, source):
        return pltpu.make_async_remote_copy(
            src_ref=slabs.at[h, group], dst_ref=main_in.at[h, source],
            send_sem=s3.at[h], recv_sem=r3.at[h],
            device_id={"gz": group - 1}, device_id_type=MESH,
        )

    def copy3_rim(h, group, source, row_to, depth_to):
        return pltpu.make_async_remote_copy(
            src_ref=slabs.at[h, group], dst_ref=rim_in.at[h, source],
            send_sem=s3.at[h], recv_sem=r3x.at[h],
            device_id={"gy": row_to, "gz": depth_to}, device_id_type=MESH,
        )

    before, after = lax.rem(gy + GY - 1, GY), lax.rem(gy + 1, GY)

    for h in range(2):
        for x in range(HX):
            for k in range(4):
                at = h * HX + x
                total = amps[k, at : at + 1, :] * along_y[0]
                for j in range(1, 4):
                    total = total + amps[j * 4 + k, at : at + 1, :] * along_y[j]
                high, low = halves(total)
                t_hi[x * 48 : (x + 1) * 48, k * SLOTS : (k + 1) * SLOTS] = high
                t_lo[x * 48 : (x + 1) * 48, k * SLOTS : (k + 1) * SLOTS] = low
        block = dot3((t_hi[...], t_lo[...]), z_all, NT)
        for x in range(HX):
            for g in range(GROUPS):
                at = x * 48 + g * 8
                slabs[h, g, x * 8 : (x + 1) * 8, :] = block[at : at + 8, :128]
                slabs[h, g, 32 + x : 33 + x, :] = jnp.sum(
                    jnp.where(keep, block[at : at + 8, 128:], 0.0), axis=0, keepdims=True
                )
        copy3(h, 3 - 2 * half + core, gz).start()
        copy3(h, 4 - 2 * half - core, gz).start()
        copy3_rim(h, 0, gz, before, GZ - 1).start()
        copy3_rim(h, 5, gz, after, 0).start()
        copy3(h, 2 + 2 * half - core, gz).start()
        main_in[h, gz] = slabs[h, 1 + gz]

    edge = (gz == 0) | (gz == GZ - 1)

    @pl.when(jnp.logical_not(edge))
    def _():
        rim_in[...] = jnp.zeros((2, GZ, SLAB, 128), F32)

    wz_copy.wait()
    wxy_copy.wait()

    def copy4(h, target, source):
        return pltpu.make_async_remote_copy(
            src_ref=out4.at[h, target],
            dst_ref=in4.at[h, pl.ds(pl.multiple_of(source * 8, 8), 8), :],
            send_sem=s4.at[h], recv_sem=r4.at[h],
            device_id=ring_peer(target), device_id_type=MESH,
        )

    def copy5(h, target, source):
        return pltpu.make_async_remote_copy(
            src_ref=out5.at[h, pl.ds(pl.multiple_of(target * 8, 8), 8), :],
            dst_ref=in5.at[h, source],
            send_sem=s5.at[h], recv_sem=r5.at[h],
            device_id=plane_peer(target), device_id_type=MESH,
        )

    def copy_d(target, source):
        return pltpu.make_async_remote_copy(
            src_ref=lines.at[target], dst_ref=dens_in.at[source],
            send_sem=sd, recv_sem=rd,
            device_id={"gz": target}, device_id_type=MESH,
        )

    row_lane = iota((32, 128), 1)
    keep_rows = row_lane // 16 == iota((32, 128), 0) % 8
    for h in range(2):
        arrived(main_in.at[h, 0 : GZ - 1], r3.at[h])

        @pl.when(edge)
        def _():
            arrived(rim_in.at[h], r3x.at[h])

        rims = []
        for q in range(GZ):
            packed = main_in[h, q, 32:SLAB, :] + rim_in[h, q, 32:SLAB, :]
            spread = jnp.concatenate(
                [jnp.broadcast_to(packed[x : x + 1], (8, 128)) for x in range(HX)], 0
            )
            spread = jnp.where(keep_rows, spread, 0.0)
            for shift in (16, 32, 64):
                spread = spread + pltpu.roll(spread, shift, 1)
            rims.append(spread)
        for q in range(GZ):
            lines[q, h * 32 : (h + 1) * 32, :] = (
                main_in[h, q, 0:32, :]
                + rim_in[h, q, 0:32, :]
                + jnp.where(row_lane >= CZ - HALO, rims[(q + 1) % GZ], 0.0)
                + jnp.where(row_lane < HALO, rims[(q + GZ - 1) % GZ], 0.0)
            )
        line_parts = halves(
            jnp.concatenate([lines[q, h * 32 : (h + 1) * 32, :] for q in range(GZ)], 1)
        )
        lines_hat = dot3(line_parts, (wz[0], wz[1]), NN)
        for c in range(4):
            pair = [lines_hat[:, p * 512 + c * 128 : p * 512 + (c + 1) * 128] for p in range(2)]
            part = jnp.concatenate([v.reshape(HX, 8, 128) for v in pair], 0)
            out4[h, c * 8 : (c + 1) * 8] = swap_lanes(part, 8, 1)

        @unrolled(RING - 1)
        def _(i):
            copy4(h, ring_step(i), me).start()

        in4[h, pl.ds(pl.multiple_of(me * 8, 8), 8), :] = out4[h, me]

    dens_in[gz] = lines[gz]

    cosines = (wxy[0], wxy[1])
    sines = (wxy[2], wxy[3])
    real_lane = iota((NXY, 128), 1) // HX % 2 == 0
    for h in range(2):
        arrived(in4.at[h, 0 : NXY - 8], r4.at[h])

        rows_in = halves(in4[h])
        with_cos = dot3(cosines, rows_in, NN)
        with_sin = dot3(sines, rows_in, NN)
        out5[h] = with_cos + jnp.where(
            real_lane, pltpu.roll(with_sin, 128 - HX, 1), -pltpu.roll(with_sin, HX, 1)
        )

        @unrolled(GX - 1)
        def _(i):
            copy5(h, plane_step(i), gx).start()

        in5[h, gx] = out5[h, pl.ds(pl.multiple_of(gx * 8, 8), 8), :]

    @pl.loop(1, GZ)
    def _(d):
        copy_d(lax.rem(gz + d, GZ), gz).start()

    with_cos = with_sin = None
    for h in range(2):
        arrived(in5.at[h, 0 : GX - 1], r5.at[h])

        x_lines = swap_lanes(in5[h], 32, HX).reshape(16, 2, 8, 128)
        x_lines = jnp.concatenate(
            [x_lines[:, p].reshape(128, 128) for p in range(2)], 0
        )
        x_lines = halves(x_lines)
        rows = slice(h * 128, (h + 1) * 128)
        add_cos = dot3(x_lines, (wxy[4, rows], wxy[5, rows]), NN)
        add_sin = dot3(x_lines, (wxy[6, rows], wxy[7, rows]), NN)
        with_cos = add_cos if h == 0 else with_cos + add_cos
        with_sin = add_sin if h == 0 else with_sin + add_sin
    spec_ref[0] = (with_cos[:128] + with_sin[128:]).reshape(16, 8, NXY)
    spec_ref[1] = (with_cos[128:] - with_sin[:128]).reshape(16, 8, NXY)

    arrived(dens_in.at[0 : GZ - 1], rd)
    for q in range(GZ):
        dens_ref[:, q * 8 : (q + 1) * 8, :] = dens_in[q].reshape(8, 8, 128)

    arrived(out1.at[0 : GX - 1], s1)
    arrived(lines.at[0 : GZ - 1], sd)
    for h in range(2):
        arrived(out5.at[h, 0 : NXY - 8], s5.at[h])
        arrived(out4.at[h, 0 : RING - 1], s4.at[h])
        arrived(slabs.at[h, 0 : GROUPS - 1], s3.at[h])


def solution(mesh):
    wz = np.stack(np_halves(depth_matrix()))
    wxy = np.concatenate([np.stack(np_halves(m)) for m in plane_matrices()])
    vmem = pl.BlockSpec(memory_space=pltpu.VMEM)
    anywhere = pl.BlockSpec(memory_space=pl.ANY)
    dma = pltpu.SemaphoreType.DMA
    call = pl.pallas_call(
        kernel,
        out_shape=(
            jax.ShapeDtypeStruct((CX, CY, CZ), F32),
            jax.ShapeDtypeStruct((2, 16, 8, NXY), F32),
        ),
        in_specs=[vmem] * 6 + [pl.BlockSpec(memory_space=pltpu.SMEM), anywhere, anywhere],
        out_specs=(vmem, vmem),
        scratch_shapes=[
            pltpu.VMEM((2, NZ, 2 * NZ), BF16),
            pltpu.VMEM((8, NXY, NXY), BF16),
            pltpu.VMEM((GX, 8, 128), F32),
            pltpu.VMEM((GX, 8, 128), F32),
            pltpu.VMEM((16, 8, SLOTS), F32),
            pltpu.VMEM((192, 4 * SLOTS), BF16),
            pltpu.VMEM((192, 4 * SLOTS), BF16),
            pltpu.VMEM((2, GROUPS, SLAB, 128), F32),
            pltpu.VMEM((2, GZ, SLAB, 128), F32),
            pltpu.VMEM((2, GZ, SLAB, 128), F32),
            pltpu.VMEM((GZ, 64, 128), F32),
            pltpu.VMEM((2, RING, 8, 128), F32),
            pltpu.VMEM((2, NXY, 128), F32),
            pltpu.VMEM((2, NXY, 128), F32),
            pltpu.VMEM((2, GX, 8, 128), F32),
            pltpu.VMEM((GZ, 64, 128), F32),
            dma((2,)),
            dma, dma,
            dma((2,)), dma((2,)), dma((2,)),
            dma((2,)), dma((2,)),
            dma((2,)), dma((2,)),
            dma, dma,
        ],
        compiler_params=pltpu.CompilerParams(collective_id=0, has_side_effects=True),
        name="pair_grid_transform",
    )

    def shards(blocks, basis, cells, offsets, eidx, ridx, exps):
        return call(
            blocks.T, basis.T, cells, offsets, eidx.reshape(1, -1), ridx.reshape(1, -1), exps,
            jnp.asarray(wz), jnp.asarray(wxy),
        )

    split = ("gx", "gy", "gz")
    placed = (P(None, split), P(), P(None, split), P(None, split), P(split), P(split), P())
    return jax.shard_map(
        shards,
        mesh=mesh,
        in_specs=placed,
        out_specs=(P("gx", "gy", "gz"), P(None, ("gy", "gz"), "gx", None)),
        check_vma=False,
    )
```

time: 80.2 us -> 75.1 us (0.936); the launches traced: 80 us -> 74.1 us
  Pallas kernels: 76.1 us -> 70.2 us
    pallas_call x1, Pallas kernels: 76.1 us -> 70.2 us  [shards(): call(blocks.T, basis.T, cells, offsets, eidx.reshape(1, -1), ridx.reshape...]
where the time goes in v2:
time: 75.1 us; the launch traced here: 74.1 us
  Pallas kernels  70.2 us (93%)
  local copies, waits for them, and re-layouts  3.24 us (4%)
    pallas_call x1, Pallas kernels, shards(): call(blocks.T, basis.T, cells, offsets, eidx.reshape(1, -1), ridx.reshape...  70.2 us
    unnamed x2, local copies, waits for them, and re-layouts  3.24 us

profile of v2, /device:TPU:1, one launch (start us, length us, event | category | flops | bytes accessed | tf_op | source)
XLA Modules:
  0.0 74.1 jit_solution(9398331272015214015)
XLA Ops:
  0.6 70.2 %pair_grid_transform.1 = (f32[8,32,128]{2,1,0:T(8,128)}, f32[2,16,8,256]{3,2,1,0:T(8,128)}) custom-call(f32[32,529]{1,0:T(8,128)} %bitcast.5, f32[64,529]{1,0:T(8,128)} %bitcast.4, s32[3,32]{1,0:T(4,128)} %cells_ref.1, f32[3,32]{1,0:T(4,128)} %offsets_ref.1, s32[1,32]{1,0:T(1,128)} %bitcast.6, s32[1,32]{1,0:T(1,128)} %bitcast.7, f32[16]{0:T(128)} %exps_ref.1, ...), custom_call_target="tpu_custom_call" | custom-call | tf_op jit(solution)/shard_map/pair_grid_transform/pallas_call | solution.py:440
  70.9 1.6 %copy.13 = f32[8,32,128]{2,1,0:T(8,128)} copy(f32[8,32,128]{2,1,0:T(8,128)} %get-tuple-element.4) | data formatting | bytes 262144
  72.4 1.7 %copy.14 = f32[2,16,8,256]{3,2,1,0:T(8,128)} copy(f32[2,16,8,256]{3,2,1,0:T(8,128)} %get-tuple-element.5) | data formatting | bytes 524288

commit v3 on v2

--- a/solution.py
+++ b/solution.py
@@ -19,6 +19,7 @@
 GROUPS = 6
 SLAB = 36
 HX = 4
+NPOLY = 64
 MESH = pl.DeviceIdType.MESH
 F32 = jnp.float32
 BF16 = jnp.bfloat16
@@ -96,10 +97,11 @@
 
 
 def kernel(
-    blocks_ref, basis_ref, cells_ref, offsets_ref, eidx_ref, ridx_ref, exps_ref,
-    wz_hbm, wxy_hbm, dens_ref, spec_ref,
+    blocks_hbm, basis_hbm, cells_hbm, offsets_hbm, eidx_hbm, ridx_hbm, exps_ref,
+    wz_hbm, wxy_hbm, dens_in, in5,
+    blocks_ref, basis_ref, cells_ref, offsets_ref, eidx_ref, ridx_ref,
     wz, wxy, out1, recv1, amps, t_hi, t_lo, slabs, main_in, rim_in, lines,
-    out4, in4, out5, in5, dens_in,
+    out4, in4, out5,
     wsem, s1, r1, s3, r3, r3x, s4, r4, s5, r5, sd, rd,
 ):
     gx, gy, gz = lax.axis_index("gx"), lax.axis_index("gy"), lax.axis_index("gz")
@@ -127,6 +129,15 @@
     def ring_peer(target):
         return {"gy": target >> 2, "gz": target & 3}
 
+    loads = [
+        pltpu.make_async_copy(source, target, wsem.at[2 + n])
+        for n, (source, target) in enumerate((
+            (blocks_hbm, blocks_ref), (basis_hbm, basis_ref), (cells_hbm, cells_ref),
+            (offsets_hbm, offsets_ref), (eidx_hbm, eidx_ref), (ridx_hbm, ridx_ref),
+        ))
+    ]
+    for load in loads:
+        load.start()
     wz_copy = pltpu.make_async_copy(wz_hbm, wz, wsem.at[0])
     wxy_copy = pltpu.make_async_copy(wxy_hbm, wxy, wsem.at[1])
     wz_copy.start()
@@ -146,6 +157,8 @@
             barrier, inc=1, device_id=ring_peer(ring_step(i)), device_id_type=MESH
         )
 
+    for load in loads:
+        load.wait()
     coefs = dot3(halves(basis_ref[...]), halves(blocks_ref[...]), NT)
     cells = cells_ref[...].astype(F32)
     radius = (HALO - ridx_ref[...]).astype(F32)
@@ -365,52 +378,60 @@
     def _(d):
         copy_d(lax.rem(gz + d, GZ), gz).start()
 
+    for h in range(2):
+        arrived(in5.at[h, 0 : GX - 1], r5.at[h])
+    arrived(dens_in.at[0 : GZ - 1], rd)
+    arrived(out1.at[0 : GX - 1], s1)
+    arrived(lines.at[0 : GZ - 1], sd)
+    for h in range(2):
+        arrived(out5.at[h, 0 : NXY - 8], s5.at[h])
+        arrived(out4.at[h, 0 : RING - 1], s4.at[h])
+        arrived(slabs.at[h, 0 : GROUPS - 1], s3.at[h])
+
+
+def last_kernel(dens_in, in5, wx, dens_ref, spec_ref):
     with_cos = with_sin = None
     for h in range(2):
-        arrived(in5.at[h, 0 : GX - 1], r5.at[h])
-
         x_lines = swap_lanes(in5[h], 32, HX).reshape(16, 2, 8, 128)
         x_lines = jnp.concatenate(
             [x_lines[:, p].reshape(128, 128) for p in range(2)], 0
         )
         x_lines = halves(x_lines)
         rows = slice(h * 128, (h + 1) * 128)
-        add_cos = dot3(x_lines, (wxy[4, rows], wxy[5, rows]), NN)
-        add_sin = dot3(x_lines, (wxy[6, rows], wxy[7, rows]), NN)
+        add_cos = dot3(x_lines, (wx[0, rows], wx[1, rows]), NN)
+        add_sin = dot3(x_lines, (wx[2, rows], wx[3, rows]), NN)
         with_cos = add_cos if h == 0 else with_cos + add_cos
         with_sin = add_sin if h == 0 else with_sin + add_sin
     spec_ref[0] = (with_cos[:128] + with_sin[128:]).reshape(16, 8, NXY)
     spec_ref[1] = (with_cos[128:] - with_sin[:128]).reshape(16, 8, NXY)
-
-    arrived(dens_in.at[0 : GZ - 1], rd)
     for q in range(GZ):
         dens_ref[:, q * 8 : (q + 1) * 8, :] = dens_in[q].reshape(8, 8, 128)
-
-    arrived(out1.at[0 : GX - 1], s1)
-    arrived(lines.at[0 : GZ - 1], sd)
-    for h in range(2):
-        arrived(out5.at[h, 0 : NXY - 8], s5.at[h])
-        arrived(out4.at[h, 0 : RING - 1], s4.at[h])
-        arrived(slabs.at[h, 0 : GROUPS - 1], s3.at[h])
 
 
 def solution(mesh):
     wz = np.stack(np_halves(depth_matrix()))
     wxy = np.concatenate([np.stack(np_halves(m)) for m in plane_matrices()])
+    wxy, wx = wxy[:4], wxy[4:]
     vmem = pl.BlockSpec(memory_space=pltpu.VMEM)
-    anywhere = pl.BlockSpec(memory_space=pl.ANY)
+    far = pl.BlockSpec(memory_space=pltpu.HBM)
     dma = pltpu.SemaphoreType.DMA
     call = pl.pallas_call(
         kernel,
         out_shape=(
-            jax.ShapeDtypeStruct((CX, CY, CZ), F32),
-            jax.ShapeDtypeStruct((2, 16, 8, NXY), F32),
+            pltpu.VMEM((GZ, 64, 128), F32),
+            pltpu.VMEM((2, GX, 8, 128), F32),
         ),
-        in_specs=[vmem] * 6 + [pl.BlockSpec(memory_space=pltpu.SMEM), anywhere, anywhere],
+        in_specs=[far] * 6 + [pl.BlockSpec(memory_space=pltpu.SMEM), far, far],
         out_specs=(vmem, vmem),
         scratch_shapes=[
+            pltpu.VMEM((32, 529), F32),
+            pltpu.VMEM((NPOLY, 529), F32),
+            pltpu.VMEM((3, 32), jnp.int32),
+            pltpu.VMEM((3, 32), F32),
+            pltpu.VMEM((1, 32), jnp.int32),
+            pltpu.VMEM((1, 32), jnp.int32),
             pltpu.VMEM((2, NZ, 2 * NZ), BF16),
-            pltpu.VMEM((8, NXY, NXY), BF16),
+            pltpu.VMEM((4, NXY, NXY), BF16),
             pltpu.VMEM((GX, 8, 128), F32),
             pltpu.VMEM((GX, 8, 128), F32),
             pltpu.VMEM((16, 8, SLOTS), F32),
@@ -423,9 +444,7 @@
             pltpu.VMEM((2, RING, 8, 128), F32),
             pltpu.VMEM((2, NXY, 128), F32),
             pltpu.VMEM((2, NXY, 128), F32),
-            pltpu.VMEM((2, GX, 8, 128), F32),
-            pltpu.VMEM((GZ, 64, 128), F32),
-            dma((2,)),
+            dma((8,)),
             dma, dma,
             dma((2,)), dma((2,)), dma((2,)),
             dma((2,)), dma((2,)),
@@ -435,12 +454,24 @@
         compiler_params=pltpu.CompilerParams(collective_id=0, has_side_effects=True),
         name="pair_grid_transform",
     )
+    last = pl.pallas_call(
+        last_kernel,
+        out_shape=(
+            jax.ShapeDtypeStruct((CX, CY, CZ), F32),
+            jax.ShapeDtypeStruct((2, 16, 8, NXY), F32),
+        ),
+        in_specs=[vmem] * 3,
+        out_specs=(vmem, vmem),
+        compiler_params=pltpu.CompilerParams(vmem_limit_bytes=16 * 1024 * 1024),
+        name="x_transform",
+    )
 
     def shards(blocks, basis, cells, offsets, eidx, ridx, exps):
-        return call(
+        dens, lines = call(
             blocks.T, basis.T, cells, offsets, eidx.reshape(1, -1), ridx.reshape(1, -1), exps,
             jnp.asarray(wz), jnp.asarray(wxy),
         )
+        return last(dens, lines, jnp.asarray(wx))
 
     split = ("gx", "gy", "gz")
     placed = (P(None, split), P(), P(None, split), P(None, split), P(split), P(split), P())

time: 75.1 us -> 72.5 us (0.965)
  local copies, waits for them, and re-layouts: 3.24 us -> 0.01 us
    unnamed x2, local copies, waits for them, and re-layouts: 3.24 us -> 0.01 us
    pallas_call x0 -> x1, Pallas kernels: none -> 1.73 us  [shards(): return last(dens, lines, jnp.asarray(wx))]
    pallas_call x1, Pallas kernels: 70.2 us -> 69.2 us  [shards(): call(blocks.T, basis.T, cells, offsets, eidx.reshape(1, -1), ridx.reshape...]
where the time goes in v3:
time: 72.5 us; the launch traced here: 71.6 us
  Pallas kernels  70.9 us (98%)
    pallas_call x1, Pallas kernels, shards(): call(blocks.T, basis.T, cells, offsets, eidx.reshape(1, -1), ridx.reshape...  69.2 us
    pallas_call x1, Pallas kernels, shards(): return last(dens, lines, jnp.asarray(wx))  1.73 us

profile of v3, /device:TPU:1, one launch (start us, length us, event | category | flops | bytes accessed | tf_op | source)
XLA Modules:
  0.0 71.6 jit_solution(8173741460002630042)
XLA Ops:
  0.6 0.0 copy-start
  0.6 69.2 %pair_grid_transform.1 = (f32[4,64,128]{2,1,0:T(8,128)S(1)}, f32[2,32,8,128]{3,2,1,0:T(8,128)S(1)}) custom-call(f32[32,529]{1,0:T(8,128)} %bitcast.5, f32[64,529]{1,0:T(8,128)} %bitcast.4, s32[3,32]{1,0:T(4,128)} %cells_hbm.1, f32[3,32]{1,0:T(4,128)} %offsets_hbm.1, s32[1,32]{1,0:T(1,128)} %bitcast.6, s32[1,32]{1,0:T(1,128)} %bitcast.7, f32[16]{0:T(128)} %exps_ref.1, ...), custom_call_target="tpu_custom_call" | custom-call | tf_op jit(solution)/shard_map/pair_grid_transform/pallas_call | solution.py:470
  69.8 0.0 copy-done
  69.8 1.7 %x_transform.1 = (f32[8,32,128]{2,1,0:T(8,128)}, f32[2,16,8,256]{3,2,1,0:T(8,128)}) custom-call(f32[4,64,128]{2,1,0:T(8,128)S(1)} %get-tuple-element.4.dens_in, f32[2,32,8,128]{3,2,1,0:T(8,128)S(1)} %get-tuple-element.5.in5, bf16[4,256,256]{2,1,0:T(8,128)(2,1)S(1)} %copy-done), custom_call_target="tpu_custom_call" | custom-call | tf_op jit(solution)/shard_map/x_transform/pallas_call | solution.py:474
Async XLA Ops:
  0.6 69.2 %copy-start = (bf16[4,256,256]{2,1,0:T(8,128)(2,1)S(1)}, bf16[4,256,256]{2,1,0:T(8,128)(2,1)}, u32[]{:S(2)}) copy-start(bf16[4,256,256]{2,1,0:T(8,128)(2,1)} %constant.8.clone.wx) | copy-start | bytes 1572868

commit v4 on v3

--- a/solution.py
+++ b/solution.py
@@ -374,9 +374,10 @@
 
         in5[h, gx] = out5[h, pl.ds(pl.multiple_of(gx * 8, 8), 8), :]
 
-    @pl.loop(1, GZ)
-    def _(d):
-        copy_d(lax.rem(gz + d, GZ), gz).start()
+        if h == 0:
+            copy_d(2 - 2 * half + core, gz).start()
+            copy_d(3 - 2 * half - core, gz).start()
+            copy_d(2 * half + 1 - core, gz).start()
 
     for h in range(2):
         arrived(in5.at[h, 0 : GX - 1], r5.at[h])

time: 72.5 us -> 69.5 us (0.959)
  Pallas kernels: 70.9 us -> 67.6 us
    pallas_call x1, Pallas kernels: 69.2 us -> 65.8 us  [shards(): call(blocks.T, basis.T, cells, offsets, eidx.reshape(1, -1), ridx.reshape...]
where the time goes in v4:
time: 69.5 us; the launch traced here: 68.2 us
  Pallas kernels  67.6 us (97%)
    pallas_call x1, Pallas kernels, shards(): call(blocks.T, basis.T, cells, offsets, eidx.reshape(1, -1), ridx.reshape...  65.8 us
    pallas_call x1, Pallas kernels, shards(): return last(dens, lines, jnp.asarray(wx))  1.74 us

profile of v4, /device:TPU:1, one launch (start us, length us, event | category | flops | bytes accessed | tf_op | source)
XLA Modules:
  0.0 68.2 jit_solution(15944989157631970277)
XLA Ops:
  0.6 0.0 copy-start
  0.6 65.8 %pair_grid_transform.1 = (f32[4,64,128]{2,1,0:T(8,128)S(1)}, f32[2,32,8,128]{3,2,1,0:T(8,128)S(1)}) custom-call(f32[32,529]{1,0:T(8,128)} %bitcast.5, f32[64,529]{1,0:T(8,128)} %bitcast.4, s32[3,32]{1,0:T(4,128)} %cells_hbm.1, f32[3,32]{1,0:T(4,128)} %offsets_hbm.1, s32[1,32]{1,0:T(1,128)} %bitcast.6, s32[1,32]{1,0:T(1,128)} %bitcast.7, f32[16]{0:T(128)} %exps_ref.1, ...), custom_call_target="tpu_custom_call" | custom-call | tf_op jit(solution)/shard_map/pair_grid_transform/pallas_call | solution.py:471
  66.5 0.0 copy-done
  66.5 1.7 %x_transform.1 = (f32[8,32,128]{2,1,0:T(8,128)}, f32[2,16,8,256]{3,2,1,0:T(8,128)}) custom-call(f32[4,64,128]{2,1,0:T(8,128)S(1)} %get-tuple-element.4.dens_in, f32[2,32,8,128]{3,2,1,0:T(8,128)S(1)} %get-tuple-element.5.in5, bf16[4,256,256]{2,1,0:T(8,128)(2,1)S(1)} %copy-done), custom_call_target="tpu_custom_call" | custom-call | tf_op jit(solution)/shard_map/x_transform/pallas_call | solution.py:475
Async XLA Ops:
  0.6 65.9 %copy-start = (bf16[4,256,256]{2,1,0:T(8,128)(2,1)S(1)}, bf16[4,256,256]{2,1,0:T(8,128)(2,1)}, u32[]{:S(2)}) copy-start(bf16[4,256,256]{2,1,0:T(8,128)(2,1)} %constant.8.clone.wx) | copy-start | bytes 1572868

commit v5 on v4

--- a/solution.py
+++ b/solution.py
@@ -57,13 +57,14 @@
     return high, (value - high.astype(np.float32)).astype(ml_dtypes.bfloat16)
 
 
-def depth_matrix():
+def depth_matrices():
     lane = np.arange(128)
-    kz = 16 * (8 * np.arange(4)[:, None] + lane[None, :] % 8) + lane[None, :] // 8
-    phase = np.arange(NZ)[:, None] * kz.reshape(-1)[None, :] % NZ
-    angle = phase * (2.0 * math.pi / NZ)
+    even = 16 * (16 * np.arange(2)[:, None] + lane[None, :] % 16) + lane[None, :] // 16 * 2
     scale = 1.0 / math.sqrt(NZ)
-    return np.concatenate([np.cos(angle) * scale, -np.sin(angle) * scale], 1)
+    for parity in range(2):
+        phase = np.arange(NZ // 2)[:, None] * (even + parity).reshape(-1)[None, :] % NZ
+        angle = phase * (2.0 * math.pi / NZ)
+        yield np.concatenate([np.cos(angle) * scale, -np.sin(angle) * scale], 1)
 
 
 def plane_matrices():
@@ -100,7 +101,7 @@
     blocks_hbm, basis_hbm, cells_hbm, offsets_hbm, eidx_hbm, ridx_hbm, exps_ref,
     wz_hbm, wxy_hbm, dens_in, in5,
     blocks_ref, basis_ref, cells_ref, offsets_ref, eidx_ref, ridx_ref,
-    wz, wxy, out1, recv1, amps, t_hi, t_lo, slabs, main_in, rim_in, lines,
+    wz, wxy, out1, recv1, arrivals, amps, t_hi, t_lo, slabs, main_in, rim_in, lines,
     out4, in4, out5,
     wsem, s1, r1, s3, r3, r3x, s4, r4, s5, r5, sd, rd,
 ):
@@ -128,6 +129,20 @@
 
     def ring_peer(target):
         return {"gy": target >> 2, "gz": target & 3}
+
+    barrier = pltpu.get_barrier_semaphore()
+
+    @unrolled(RING - 1)
+    def _(i):
+        pl.semaphore_signal(
+            barrier, inc=1, device_id=ring_peer(ring_step(i)), device_id_type=MESH
+        )
+
+    @unrolled(GX - 1)
+    def _(i):
+        pl.semaphore_signal(
+            barrier, inc=1, device_id=plane_peer(plane_step(i)), device_id_type=MESH
+        )
 
     loads = [
         pltpu.make_async_copy(source, target, wsem.at[2 + n])
@@ -142,20 +157,6 @@
     wxy_copy = pltpu.make_async_copy(wxy_hbm, wxy, wsem.at[1])
     wz_copy.start()
     wxy_copy.start()
-
-    barrier = pltpu.get_barrier_semaphore()
-
-    @unrolled(GX - 1)
-    def _(i):
-        pl.semaphore_signal(
-            barrier, inc=1, device_id=plane_peer(plane_step(i)), device_id_type=MESH
-        )
-
-    @unrolled(RING - 1)
-    def _(i):
-        pl.semaphore_signal(
-            barrier, inc=1, device_id=ring_peer(ring_step(i)), device_id_type=MESH
-        )
 
     for load in loads:
         load.wait()
@@ -177,15 +178,29 @@
     earlier = (owner_column == owner) & (iota((32, 32), 0) < iota((32, 32), 1))
     within = jnp.sum(jnp.where(earlier, 1.0, 0.0), axis=0, keepdims=True).astype(jnp.int32)
     base = owner * 2 + within
-    row = iota((SLOTS, 1), 0)
-    slot = row % 8
-    code = (row // 8 + slot // 2 + (GX - 1)) % GX * 2 + slot % 2
-    code = jnp.where(slot < 6, code, -1)
-    pick = jnp.where(code == base, 1.0, 0.0).astype(BF16)
-    high, middle = halves(data)
-    rest = (data - high.astype(F32) - middle.astype(F32)).astype(BF16)
-    routed = dot(pick, high, NT) + dot(pick, middle, NT) + dot(pick, rest, NT)
-    out1[...] = routed.reshape(GX, 8, 128)
+    row = iota((4 * GX, 1), 0)
+    turn = row % 4
+    pieces = halves(data)
+    rest = (data - pieces[0].astype(F32) - pieces[1].astype(F32)).astype(BF16)
+    chosen = []
+    for side in range(2):
+        code = (row // 4 + turn + (GX - 1)) % GX * 2 + side
+        code = jnp.where(turn < 3, code, -1)
+        pick = jnp.where(code == base, 1.0, 0.0).astype(BF16)
+        chosen.append(
+            dot(pick, pieces[0], NT) + dot(pick, pieces[1], NT) + dot(pick, rest, NT)
+        )
+    lane = iota((4 * GX, 128), 1)
+    packed = jnp.where(lane < 64, chosen[0], pltpu.roll(chosen[1], 64, 1))
+    labels = jnp.zeros((4 * GX, 128), F32)
+    for r in range(3):
+        for side in range(2):
+            spot = r * 16 + side * 8
+            moved = pltpu.roll(pltpu.roll(chosen[side], 64 + spot, 1), 3 - r, 0)
+            labels = jnp.where((lane >= spot) & (lane < spot + 8), moved, labels)
+    packed = jnp.where(iota((4 * GX, 128), 0) % 4 == 3, labels, packed)
+    for target in range(GX):
+        out1[target] = packed[target * 4 : (target + 1) * 4, :]
     recv1[gx] = out1[gx]
 
     pl.semaphore_wait(barrier, GX + RING - 2)
@@ -203,10 +218,25 @@
 
     arrived(recv1.at[0 : GX - 1], r1)
 
-    table = recv1[...].reshape(SLOTS, 128).T
-    cx, cy, cz = table[64:65], table[65:66], table[66:67]
-    ox, oy, oz = table[67:68], table[68:69], table[69:70]
-    rates, radii = table[70:71], table[71:72]
+    for source in range(GX):
+        arrivals[source * 4 : (source + 1) * 4, :] = recv1[source]
+    turned = arrivals[...].T
+    column = iota((1, 128), 1) % 4
+    table = jnp.concatenate(
+        [jnp.where(column < 3, turned[side * 64 : side * 64 + 64], 0.0) for side in range(2)], 1
+    )
+    labels = []
+    for side in range(2):
+        own = jnp.zeros((8, 128), F32)
+        for r in range(3):
+            spot = r * 16 + side * 8
+            moved = pltpu.roll(turned[spot : spot + 8], 125 + r, 1)
+            own = jnp.where(column == r, moved, own)
+        labels.append(own)
+    labels = jnp.concatenate(labels, 1)
+    cx, cy, cz = labels[0:1], labels[1:2], labels[2:3]
+    ox, oy, oz = labels[3:4], labels[4:5], labels[5:6]
+    rates, radii = labels[6:7], labels[7:8]
 
     def factors(offset_cells, offset_in):
         distance = offset_cells - offset_in
@@ -338,14 +368,21 @@
                 + jnp.where(row_lane >= CZ - HALO, rims[(q + 1) % GZ], 0.0)
                 + jnp.where(row_lane < HALO, rims[(q + GZ - 1) % GZ], 0.0)
             )
-        line_parts = halves(
-            jnp.concatenate([lines[q, h * 32 : (h + 1) * 32, :] for q in range(GZ)], 1)
-        )
-        lines_hat = dot3(line_parts, (wz[0], wz[1]), NN)
-        for c in range(4):
-            pair = [lines_hat[:, p * 512 + c * 128 : p * 512 + (c + 1) * 128] for p in range(2)]
-            part = jnp.concatenate([v.reshape(HX, 8, 128) for v in pair], 0)
-            out4[h, c * 8 : (c + 1) * 8] = swap_lanes(part, 8, 1)
+        near = [lines[q, h * 32 : (h + 1) * 32, :] for q in range(GZ)]
+        sums = jnp.concatenate([near[0] + near[2], near[1] + near[3]], 1)
+        gaps = jnp.concatenate([near[0] - near[2], near[1] - near[3]], 1)
+        even = dot3(halves(sums), (wz[0], wz[1]), NN)
+        odd = dot3(halves(gaps), (wz[2], wz[3]), NN)
+        for c in range(2):
+            part = jnp.concatenate(
+                [
+                    v[:, p * 256 + c * 128 : p * 256 + (c + 1) * 128].reshape(HX, 8, 128)
+                    for v in (even, odd)
+                    for p in range(2)
+                ],
+                0,
+            )
+            out4[h, c * 16 : (c + 1) * 16] = swap_lanes(part, 16, 1)
 
         @unrolled(RING - 1)
         def _(i):
@@ -410,7 +447,7 @@
 
 
 def solution(mesh):
-    wz = np.stack(np_halves(depth_matrix()))
+    wz = np.concatenate([np.stack(np_halves(m)) for m in depth_matrices()])
     wxy = np.concatenate([np.stack(np_halves(m)) for m in plane_matrices()])
     wxy, wx = wxy[:4], wxy[4:]
     vmem = pl.BlockSpec(memory_space=pltpu.VMEM)
@@ -431,10 +468,11 @@
             pltpu.VMEM((3, 32), F32),
             pltpu.VMEM((1, 32), jnp.int32),
             pltpu.VMEM((1, 32), jnp.int32),
-            pltpu.VMEM((2, NZ, 2 * NZ), BF16),
+            pltpu.VMEM((4, NZ // 2, NZ), BF16),
             pltpu.VMEM((4, NXY, NXY), BF16),
-            pltpu.VMEM((GX, 8, 128), F32),
-            pltpu.VMEM((GX, 8, 128), F32),
+            pltpu.VMEM((GX, 4, 128), F32),
+            pltpu.VMEM((GX, 4, 128), F32),
+            pltpu.VMEM((4 * GX, 128), F32),
             pltpu.VMEM((16, 8, SLOTS), F32),
             pltpu.VMEM((192, 4 * SLOTS), BF16),
             pltpu.VMEM((192, 4 * SLOTS), BF16),

time: 69.5 us -> 68.3 us (0.983); the launches traced: 68.2 us -> 68.1 us
  no operation moved by 1% of the time
where the time goes in v5:
time: 68.3 us; the launch traced here: 68.1 us
  Pallas kernels  67.5 us (99%)
    pallas_call x1, Pallas kernels, shards(): call(blocks.T, basis.T, cells, offsets, eidx.reshape(1, -1), ridx.reshape...  65.7 us
    pallas_call x1, Pallas kernels, shards(): return last(dens, lines, jnp.asarray(wx))  1.74 us

profile of v5, /device:TPU:1, one launch (start us, length us, event | category | flops | bytes accessed | tf_op | source)
XLA Modules:
  0.0 68.1 jit_solution(5357187694636749617)
XLA Ops:
  0.6 0.0 copy-start
  0.6 65.7 %pair_grid_transform.1 = (f32[4,64,128]{2,1,0:T(8,128)S(1)}, f32[2,32,8,128]{3,2,1,0:T(8,128)S(1)}) custom-call(f32[32,529]{1,0:T(8,128)} %bitcast.5, f32[64,529]{1,0:T(8,128)} %bitcast.4, s32[3,32]{1,0:T(4,128)} %cells_hbm.1, f32[3,32]{1,0:T(4,128)} %offsets_hbm.1, s32[1,32]{1,0:T(1,128)} %bitcast.6, s32[1,32]{1,0:T(1,128)} %bitcast.7, f32[16]{0:T(128)} %exps_ref.1, ...), custom_call_target="tpu_custom_call" | custom-call | tf_op jit(solution)/shard_map/pair_grid_transform/pallas_call | solution.py:509
  66.4 0.0 copy-done
  66.4 1.7 %x_transform.1 = (f32[8,32,128]{2,1,0:T(8,128)}, f32[2,16,8,256]{3,2,1,0:T(8,128)}) custom-call(f32[4,64,128]{2,1,0:T(8,128)S(1)} %get-tuple-element.4.dens_in, f32[2,32,8,128]{3,2,1,0:T(8,128)S(1)} %get-tuple-element.5.in5, bf16[4,256,256]{2,1,0:T(8,128)(2,1)S(1)} %copy-done), custom_call_target="tpu_custom_call" | custom-call | tf_op jit(solution)/shard_map/x_transform/pallas_call | solution.py:513
Async XLA Ops:
  0.6 65.8 %copy-start = (bf16[4,256,256]{2,1,0:T(8,128)(2,1)S(1)}, bf16[4,256,256]{2,1,0:T(8,128)(2,1)}, u32[]{:S(2)}) copy-start(bf16[4,256,256]{2,1,0:T(8,128)(2,1)} %constant.8.clone.wx) | copy-start | bytes 1572868

commit v6 on v5

--- a/solution.py
+++ b/solution.py
@@ -284,6 +284,8 @@
         )
 
     before, after = lax.rem(gy + GY - 1, GY), lax.rem(gy + 1, GY)
+    far_row = jnp.where(half == 0, before, after)
+    near_row = jnp.where(half == 0, after, before)
 
     for h in range(2):
         for x in range(HX):
@@ -305,8 +307,8 @@
                 )
         copy3(h, 3 - 2 * half + core, gz).start()
         copy3(h, 4 - 2 * half - core, gz).start()
-        copy3_rim(h, 0, gz, before, GZ - 1).start()
-        copy3_rim(h, 5, gz, after, 0).start()
+        copy3_rim(h, 5 * half, gz, far_row, (1 - half) * (GZ - 1)).start()
+        copy3_rim(h, 5 - 5 * half, gz, near_row, half * (GZ - 1)).start()
         copy3(h, 2 + 2 * half - core, gz).start()
         main_in[h, gz] = slabs[h, 1 + gz]
 

time: 68.3 us -> 70.7 us (1.035)
  the two profiles are of different devices: /device:TPU:1 before, /device:TPU:3 now
where the time goes in v6:
time: 70.7 us; the launch traced here: 70.6 us
  Pallas kernels  69.9 us (99%)
    pallas_call x1, Pallas kernels, shards(): call(blocks.T, basis.T, cells, offsets, eidx.reshape(1, -1), ridx.reshape...  68.2 us
    pallas_call x1, Pallas kernels, shards(): return last(dens, lines, jnp.asarray(wx))  1.73 us

profile of v6, /device:TPU:3, one launch (start us, length us, event | category | flops | bytes accessed | tf_op | source)
XLA Modules:
  0.0 70.6 jit_solution(656028231414293906)
XLA Ops:
  0.6 0.0 copy-start
  0.6 68.2 %pair_grid_transform.1 = (f32[4,64,128]{2,1,0:T(8,128)S(1)}, f32[2,32,8,128]{3,2,1,0:T(8,128)S(1)}) custom-call(f32[32,529]{1,0:T(8,128)} %bitcast.5, f32[64,529]{1,0:T(8,128)} %bitcast.4, s32[3,32]{1,0:T(4,128)} %cells_hbm.1, f32[3,32]{1,0:T(4,128)} %offsets_hbm.1, s32[1,32]{1,0:T(1,128)} %bitcast.6, s32[1,32]{1,0:T(1,128)} %bitcast.7, f32[16]{0:T(128)} %exps_ref.1, ...), custom_call_target="tpu_custom_call" | custom-call | tf_op jit(solution)/shard_map/pair_grid_transform/pallas_call | solution.py:511
  68.8 0.0 copy-done
  68.8 1.7 %x_transform.1 = (f32[8,32,128]{2,1,0:T(8,128)}, f32[2,16,8,256]{3,2,1,0:T(8,128)}) custom-call(f32[4,64,128]{2,1,0:T(8,128)S(1)} %get-tuple-element.4.dens_in, f32[2,32,8,128]{3,2,1,0:T(8,128)S(1)} %get-tuple-element.5.in5, bf16[4,256,256]{2,1,0:T(8,128)(2,1)S(1)} %copy-done), custom_call_target="tpu_custom_call" | custom-call | tf_op jit(solution)/shard_map/x_transform/pallas_call | solution.py:515
Async XLA Ops:
  0.6 68.2 %copy-start = (bf16[4,256,256]{2,1,0:T(8,128)(2,1)S(1)}, bf16[4,256,256]{2,1,0:T(8,128)(2,1)}, u32[]{:S(2)}) copy-start(bf16[4,256,256]{2,1,0:T(8,128)(2,1)} %constant.8.clone.wx) | copy-start | bytes 1572868
